TPU v7x, 32 devices: a whole 2x2x4 slice. The times are simulated.
32 devices in a mesh: depth: 4 (over y, core), blk: 8 (over z, x).
Axes of the slice: x: 2, y: 2, z: 4, core: 2. Of those that a mesh axis runs over, the one named last changes fastest.
Arguments:
- jacobian: bfloat16 [96, 16384], P(('depth', 'blk')), may hold values from -6 to 6
- gain_inverse: bfloat16 [16384, 16384], P('depth', 'blk'), may hold values from -0.00024414062 to 0.00048828125, as said below
- variance: float32 [96], P(('depth', 'blk')), may hold values from 2 to 12
Outputs:
- omega_diag: float32 [96], P(('depth', 'blk'))
Inputs may be any that keep to these rules, and one draw needn't show every extreme that they name: gain_inverse is symmetric and positive definite.
All inputs are finite; a program needn't handle non-finite values.
Results may differ from a plain program's by a relative error of at most 0.0003.
Values may be sent and summed in bfloat16 or wider, within the bound.
A program may use at most 128 MiB of HBM per device.

v0:
```python
import jax
import jax.numpy as jnp
from jax import lax
from jax.sharding import PartitionSpec as P


def shards(jacobian, gain_inverse, variance):
    rows_local = jacobian.shape[0]
    depth_count = lax.axis_size("depth")
    blk_count = lax.axis_size("blk")
    quarter_rows = lax.all_to_all(jacobian, "depth", split_axis=1, concat_axis=0, tiled=True)
    whole_rows = lax.all_gather(jacobian, "depth", axis=0, tiled=True)
    panel = lax.all_to_all(whole_rows, "blk", split_axis=1, concat_axis=0, tiled=True)
    projected = jnp.dot(
        lax.all_gather(quarter_rows, "blk", axis=0, tiled=True),
        gain_inverse,
        preferred_element_type=jnp.float32,
    )
    partial_sum = jnp.sum(projected * panel.astype(jnp.float32), axis=1)
    by_section = partial_sum.reshape(blk_count, depth_count * rows_local)
    reduced = lax.psum_scatter(by_section, "blk", scatter_dimension=0, tiled=True).reshape(-1)
    quadratic = lax.psum_scatter(reduced, "depth", scatter_dimension=0, tiled=True)
    return variance - quadratic


def solution(mesh):
    in_specs = (P(("depth", "blk"), None), P("depth", "blk"), P(("depth", "blk")))
    out_specs = P(("depth", "blk"))
    return jax.shard_map(shards, mesh=mesh, in_specs=in_specs, out_specs=out_specs, check_vma=False)
```

profile of v0, /device:TPU:0, one launch (start us, length us, event | category | flops | bytes accessed | tf_op | source)
XLA Modules:
  0.0 96.0 jit_solution(18339546582499330617)
XLA Ops:
  0.0 4.3 %all-to-all-start = ((bf16[3,4,4096]{2,0,1:T(4,128)(2,1)}), bf16[3,4,4096]{2,0,1:T(4,128)(2,1)S(1)}, u32[]{:S(2)}, u32[]{:S(2)}) async-start(bf16[3,4,4096]{2,0,1:T(4,128)(2,1)} %bitcast.11), calls=%async_computation | async-start | bytes 262144 | tf_op jit(solution)/shard_map/all_to_all | solution.py:11
  4.3 8.3 %all-gather.1 = bf16[4,3,16384]{2,1,0:T(4,128)(2,1)S(1)} all-gather(bf16[1,3,16384]{2,1,0:T(4,128)(2,1)} %bitcast.12), channel_id=1, replica_groups=mesh['depth'=4,'blk'=8] {'depth'}, dimensions={0}, use_global_device_ids=true | all-gather | bytes 491520 | tf_op jit(solution)/shard_map/all_gather | solution.py:12
  12.5 0.5 all_to_all.28
  13.1 0.0 copy-start
  13.1 1.0 %copy.8 = bf16[12,8,2048]{2,0,1:T(8,128)(2,1)} copy(bf16[12,8,2048]{2,1,0:T(8,128)(2,1)S(1)} %all_to_all.28) | data formatting | bytes 786432 | tf_op jit(solution)/shard_map/all_to_all | solution.py:13
  14.1 0.0 all-to-all-done
  14.1 6.3 %all-to-all-start.1 = ((bf16[12,8,2048]{2,0,1:T(8,128)(2,1)}), bf16[12,8,2048]{2,0,1:T(8,128)(2,1)S(1)}, u32[]{:S(2)}, u32[]{:S(2)}) async-start(bf16[12,8,2048]{2,0,1:T(8,128)(2,1)} %copy.8), calls=%async_computation.1 | async-start | bytes 1048576 | tf_op jit(solution)/shard_map/all_to_all | solution.py:13
  20.4 1.2 %dynamic-slice = u32[1]{0:T(128)} dynamic-slice(u32[32]{0:T(128)} %constant.6, u32[]{:T(128)S(6)} %add.5), dynamic_slice_sizes={1} | dynamic-slice | bytes 12
  21.7 1.3 %dynamic-slice.2 = u32[1]{0:T(128)} dynamic-slice(u32[32]{0:T(128)} %constant.10, u32[]{:T(128)S(6)} %add.5), dynamic_slice_sizes={1} | dynamic-slice | bytes 12
  23.0 0.1 reshape.17
  23.1 37.9 %all-gather = bf16[8,12,4096]{2,1,0:T(8,128)(2,1)S(1)} all-gather(bf16[1,12,4096]{2,1,0:T(8,128)(2,1)S(1)} %reshape.17), channel_id=1, replica_groups=mesh['depth'=4,'blk'=8] {'blk'}, dimensions={0}, use_global_device_ids=true | all-gather | bytes 884736 | tf_op jit(solution)/shard_map/all_gather | solution.py:15
  61.0 0.2 reshape.18
  61.1 0.0 all-to-all-done.1
  61.2 0.1 convert_bitcast_fusion
  61.3 0.1 reshape.16
  61.4 8.7 %fusion = f32[96]{0:T(128)S(1)} fusion(f32[96,2048]{1,0:T(8,128)S(1)} %reshape.16, bf16[96,4096]{1,0:T(8,128)(2,1)S(1)} %reshape.18, bf16[4096,2048]{1,0:T(8,128)(2,1)} %param.4), kind=kOutput, calls=%fused_computation.1 | convolution fusion | flops 1611005824 | bytes 18350464 | tf_op jit(solution)/shard_map/dot_general | solution.py:14
  70.0 0.1 reshape.14
  70.1 18.3 %all-reduce = f32[8,12]{1,0:T(8,128)S(1)} all-reduce(f32[8,12]{1,0:T(8,128)S(1)} %reshape.14), channel_id=2, replica_groups=mesh['depth'=4,'blk'=8] {'blk'}, use_global_device_ids=true, to_apply=%region_1.0.clone | all-reduce | flops 96 | bytes 768
  88.4 0.6 dynamic-slice_bitcast_fusion
  89.7 5.7 %all-reduce.1 = f32[12]{0:T(128)S(1)} all-reduce(f32[12]{0:T(128)S(1)} %dynamic-slice_bitcast_fusion), channel_id=3, replica_groups=mesh['depth'=4,'blk'=8] {'depth'}, use_global_device_ids=true, to_apply=%region_2.0.clone | all-reduce | flops 12 | bytes 96
  95.4 0.0 copy-done
  95.4 0.6 dynamic-slice_subtract_fusion
Async XLA Ops:
  0.0 14.1 %all-to-all-start = ((bf16[3,4,4096]{2,0,1:T(4,128)(2,1)}), bf16[3,4,4096]{2,0,1:T(4,128)(2,1)S(1)}, u32[]{:S(2)}, u32[]{:S(2)}) async-start(bf16[3,4,4096]{2,0,1:T(4,128)(2,1)} %bitcast.11), calls=%async_computation | async-start | bytes 262144 | tf_op jit(solution)/shard_map/all_to_all | solution.py:11
  13.1 82.3 %copy-start = (f32[3]{0:T(128)S(1)}, f32[3]{0:T(128)}, u32[]{:S(2)}) copy-start(f32[3]{0:T(128)} %param.5) | copy-start | bytes 40
  14.1 47.0 %all-to-all-start.1 = ((bf16[12,8,2048]{2,0,1:T(8,128)(2,1)}), bf16[12,8,2048]{2,0,1:T(8,128)(2,1)S(1)}, u32[]{:S(2)}, u32[]{:S(2)}) async-start(bf16[12,8,2048]{2,0,1:T(8,128)(2,1)} %copy.8), calls=%async_computation.1 | async-start | bytes 1048576 | tf_op jit(solution)/shard_map/all_to_all | solution.py:13
where the time goes:
time: 96.4 us; the launch traced here: 96 us
  blocking collectives  70.1 us (73%)
  starting transfers between devices  10.6 us (11%)
  matrix products  8.66 us (9%)
  local copies, waits for them, and re-layouts  5.19 us (5%)
    all_gather x1, blocking collectives, shards(): lax.all_gather(quarter_rows, 'blk', axis=0, tiled=True)  37.9 us
    unnamed x2, blocking collectives  24 us
    dot_general x1, matrix products, shards(): jnp.dot(lax.all_gather(quarter_rows, 'blk', axis=0, tiled=True), gain_inv...  8.66 us
    all_gather x1, blocking collectives, shards(): whole_rows = lax.all_gather(jacobian, 'depth', axis=0, tiled=True)  8.27 us
    all_to_all x1, starting transfers between devices, shards(): lax.all_to_all(whole_rows, 'blk', split_axis=1, concat_axis=0, tiled=True)  6.31 us
    all_to_all x1, starting transfers between devices, shards(): lax.all_to_all(jacobian, 'depth', split_axis=1, concat_axis=0, tiled=True)  4.26 us
    unnamed x6, local copies, waits for them, and re-layouts  2.82 us
  transfers between devices with their start and end apart: 2, of which 0 were waited for; matrix products, arithmetic and copies ran while one was open for 4% of the time, Pallas kernels for 0%

commit v1 on v0

--- a/solution.py
+++ b/solution.py
@@ -2,6 +2,11 @@
 import jax.numpy as jnp
 from jax import lax
 from jax.sharding import PartitionSpec as P
+
+
+def exchange_gather(x, axis, dim):
+    repeated = jnp.stack([x] * lax.axis_size(axis))
+    return jnp.concatenate(lax.all_to_all(repeated, axis, 0, 0), axis=dim)
 
 
 def shards(jacobian, gain_inverse, variance):
@@ -12,9 +17,7 @@
     whole_rows = lax.all_gather(jacobian, "depth", axis=0, tiled=True)
     panel = lax.all_to_all(whole_rows, "blk", split_axis=1, concat_axis=0, tiled=True)
     projected = jnp.dot(
-        lax.all_gather(quarter_rows, "blk", axis=0, tiled=True),
-        gain_inverse,
-        preferred_element_type=jnp.float32,
+        exchange_gather(quarter_rows, "blk", 0), gain_inverse, preferred_element_type=jnp.float32
     )
     partial_sum = jnp.sum(projected * panel.astype(jnp.float32), axis=1)
     by_section = partial_sum.reshape(blk_count, depth_count * rows_local)

time: 96.4 us -> 103 us (1.068)
  waiting for transfers between devices: 0.01 us -> 38.1 us
  blocking collectives: 70.1 us -> 33.4 us
  starting transfers between devices: 10.6 us -> 14.2 us
  local copies, waits for them, and re-layouts: 5.19 us -> 6.28 us
    all_gather x1 -> x0, blocking collectives: 37.9 us -> none  [shards(): lax.all_gather(quarter_rows, 'blk', axis=0, tiled=True)]
    all_to_all x0 -> x1, waiting for transfers between devices: none -> 23.2 us  [exchange_gather(): return jnp.concatenate(lax.all_to_all(repeated, axis, 0, 0), axis=dim)]
    all_to_all x1, waiting for transfers between devices: 0.01 us -> 14.9 us  [shards(): lax.all_to_all(whole_rows, 'blk', split_axis=1, concat_axis=0, tiled=True)]
    all_to_all x0 -> x1, starting transfers between devices: none -> 3.64 us  [exchange_gather(): return jnp.concatenate(lax.all_to_all(repeated, axis, 0, 0), axis=dim)]
    another operation x0 -> x2, local copies, waits for them, and re-layouts: none -> 1.18 us  [exchange_gather(): repeated = jnp.stack([x] * lax.axis_size(axis))]
    unnamed x2, blocking collectives: 24 us -> 25.1 us
    unnamed x6 -> x4, local copies, waits for them, and re-layouts: 2.82 us -> 2.56 us
  transfers between devices with their start and end apart: 2 -> 3, of which waited for: 0 -> 2; matrix products, arithmetic and copies ran while one was open for 4% -> 4% of each run, Pallas kernels for 0% -> 0%
where the time goes in v1:
time: 103 us; the launch traced here: 102 us
  waiting for transfers between devices  38.1 us (37%)
  blocking collectives  33.4 us (32%)
  starting transfers between devices  14.2 us (14%)
  matrix products  8.67 us (8%)
  local copies, waits for them, and re-layouts  6.28 us (6%)
    unnamed x2, blocking collectives  25.1 us
    all_to_all x1, waiting for transfers between devices, exchange_gather(): return jnp.concatenate(lax.all_to_all(repeated, axis, 0, 0), axis=dim)  23.2 us
    all_to_all x1, waiting for transfers between devices, shards(): lax.all_to_all(whole_rows, 'blk', split_axis=1, concat_axis=0, tiled=True)  14.9 us
    dot_general x1, matrix products, shards(): jnp.dot(exchange_gather(quarter_rows, 'blk', 0), gain_inverse, preferred_...  8.67 us
    all_gather x1, blocking collectives, shards(): whole_rows = lax.all_gather(jacobian, 'depth', axis=0, tiled=True)  8.27 us
    all_to_all x1, starting transfers between devices, shards(): lax.all_to_all(whole_rows, 'blk', split_axis=1, concat_axis=0, tiled=True)  6.31 us
    all_to_all x1, starting transfers between devices, shards(): lax.all_to_all(jacobian, 'depth', split_axis=1, concat_axis=0, tiled=True)  4.26 us
    all_to_all x1, starting transfers between devices, exchange_gather(): return jnp.concatenate(lax.all_to_all(repeated, axis, 0, 0), axis=dim)  3.64 us
  transfers between devices with their start and end apart: 3, of which 2 were waited for; matrix products, arithmetic and copies ran while one was open for 4% of the time, Pallas kernels for 0%

profile of v1, /device:TPU:0, one launch (start us, length us, event | category | flops | bytes accessed | tf_op | source)
XLA Modules:
  0.0 102.1 jit_solution(16660779259502395894)
XLA Ops:
  0.0 4.3 %all-to-all-start = ((bf16[3,4,4096]{2,0,1:T(4,128)(2,1)}), bf16[3,4,4096]{2,0,1:T(4,128)(2,1)S(1)}, u32[]{:S(2)}, u32[]{:S(2)}) async-start(bf16[3,4,4096]{2,0,1:T(4,128)(2,1)} %bitcast.11), calls=%async_computation | async-start | bytes 262144 | tf_op jit(solution)/shard_map/all_to_all | solution.py:16
  4.3 8.3 %all-gather = bf16[4,3,16384]{2,1,0:T(4,128)(2,1)S(1)} all-gather(bf16[1,3,16384]{2,1,0:T(4,128)(2,1)} %bitcast.12), channel_id=1, replica_groups=mesh['depth'=4,'blk'=8] {'depth'}, dimensions={0}, use_global_device_ids=true | all-gather | bytes 491520 | tf_op jit(solution)/shard_map/all_gather | solution.py:17
  12.5 0.5 all_to_all.29
  13.1 1.0 %copy.8 = bf16[12,8,2048]{2,0,1:T(8,128)(2,1)} copy(bf16[12,8,2048]{2,1,0:T(8,128)(2,1)S(1)} %all_to_all.29) | data formatting | bytes 786432 | tf_op jit(solution)/shard_map/all_to_all | solution.py:18
  14.1 0.0 all-to-all-done
  14.1 6.3 %all-to-all-start.2 = ((bf16[12,8,2048]{2,0,1:T(8,128)(2,1)}), bf16[12,8,2048]{2,0,1:T(8,128)(2,1)S(1)}, u32[]{:S(2)}, u32[]{:S(2)}) async-start(bf16[12,8,2048]{2,0,1:T(8,128)(2,1)} %copy.8), calls=%async_computation.2 | async-start | bytes 1048576 | tf_op jit(solution)/shard_map/all_to_all | solution.py:18
  20.4 0.1 stack.4
  20.5 0.0 copy-start
  20.5 14.9 %all-to-all-done.2 = bf16[12,8,2048]{2,0,1:T(8,128)(2,1)S(1)} async-done(((bf16[12,8,2048]{2,0,1:T(8,128)(2,1)}), bf16[12,8,2048]{2,0,1:T(8,128)(2,1)S(1)}, u32[]{:S(2)}, u32[]{:S(2)}) %all-to-all-start.2) | async-done | bytes 393248 | tf_op jit(solution)/shard_map/all_to_all | solution.py:18
  35.4 1.1 %stack.5 = bf16[8,12,4096]{2,1,0:T(8,128)(2,1)} broadcast(bf16[12,4096]{1,0:T(8,128)(2,1)S(1)} %stack.4), dimensions={1,2} | broadcast | bytes 884736 | tf_op jit(solution)/shard_map/stack | solution.py:8
  36.5 3.6 %all-to-all-start.1 = ((bf16[8,12,4096]{2,1,0:T(8,128)(2,1)}), bf16[8,12,4096]{2,1,0:T(8,128)(2,1)S(1)}, u32[]{:S(2)}, u32[]{:S(2)}) async-start(bf16[8,12,4096]{2,1,0:T(8,128)(2,1)} %stack.5), calls=%async_computation.1 | async-start | bytes 2097152 | tf_op jit(solution)/shard_map/all_to_all | solution.py:9
  40.1 1.2 %dynamic-slice = u32[1]{0:T(128)} dynamic-slice(u32[32]{0:T(128)} %constant.6, u32[]{:T(128)S(6)} %add.5), dynamic_slice_sizes={1} | dynamic-slice | bytes 12
  41.4 1.3 %dynamic-slice.2 = u32[1]{0:T(128)} dynamic-slice(u32[32]{0:T(128)} %constant.10, u32[]{:T(128)S(6)} %add.5), dynamic_slice_sizes={1} | dynamic-slice | bytes 12
  42.7 0.1 convert_bitcast_fusion
  42.8 0.1 reshape.23
  42.9 23.2 %all-to-all-done.1 = bf16[8,12,4096]{2,1,0:T(8,128)(2,1)S(1)} async-done(((bf16[8,12,4096]{2,1,0:T(8,128)(2,1)}), bf16[8,12,4096]{2,1,0:T(8,128)(2,1)S(1)}, u32[]{:S(2)}, u32[]{:S(2)}) %all-to-all-start.1) | async-done | bytes 786464 | tf_op jit(solution)/shard_map/all_to_all | solution.py:9
  66.1 0.2 reshape.20
  66.3 8.7 %fusion = f32[96]{0:T(128)S(1)} fusion(f32[96,2048]{1,0:T(8,128)S(1)} %reshape.23, bf16[96,4096]{1,0:T(8,128)(2,1)S(1)} %reshape.20, bf16[4096,2048]{1,0:T(8,128)(2,1)} %param.4), kind=kOutput, calls=%fused_computation.1 | convolution fusion | flops 1611005824 | bytes 18350464 | tf_op jit(solution)/shard_map/dot_general | solution.py:19
  75.0 0.1 reshape.21
  75.0 19.5 %all-reduce = f32[8,12]{1,0:T(8,128)S(1)} all-reduce(f32[8,12]{1,0:T(8,128)S(1)} %reshape.21), channel_id=2, replica_groups=mesh['depth'=4,'blk'=8] {'blk'}, use_global_device_ids=true, to_apply=%region_1.0.clone | all-reduce | flops 96 | bytes 768
  94.5 0.6 dynamic-slice_bitcast_fusion
  95.8 5.7 %all-reduce.1 = f32[12]{0:T(128)S(1)} all-reduce(f32[12]{0:T(128)S(1)} %dynamic-slice_bitcast_fusion), channel_id=3, replica_groups=mesh['depth'=4,'blk'=8] {'depth'}, use_global_device_ids=true, to_apply=%region_2.0.clone | all-reduce | flops 12 | bytes 96
  101.5 0.0 copy-done
  101.5 0.6 dynamic-slice_subtract_fusion
Async XLA Ops:
  0.0 14.1 %all-to-all-start = ((bf16[3,4,4096]{2,0,1:T(4,128)(2,1)}), bf16[3,4,4096]{2,0,1:T(4,128)(2,1)S(1)}, u32[]{:S(2)}, u32[]{:S(2)}) async-start(bf16[3,4,4096]{2,0,1:T(4,128)(2,1)} %bitcast.11), calls=%async_computation | async-start | bytes 262144 | tf_op jit(solution)/shard_map/all_to_all | solution.py:16
  14.1 21.3 %all-to-all-start.2 = ((bf16[12,8,2048]{2,0,1:T(8,128)(2,1)}), bf16[12,8,2048]{2,0,1:T(8,128)(2,1)S(1)}, u32[]{:S(2)}, u32[]{:S(2)}) async-start(bf16[12,8,2048]{2,0,1:T(8,128)(2,1)} %copy.8), calls=%async_computation.2 | async-start | bytes 1048576 | tf_op jit(solution)/shard_map/all_to_all | solution.py:18
  20.5 81.0 %copy-start = (f32[3]{0:T(128)S(1)}, f32[3]{0:T(128)}, u32[]{:S(2)}) copy-start(f32[3]{0:T(128)} %param.5) | copy-start | bytes 40
  36.5 29.6 %all-to-all-start.1 = ((bf16[8,12,4096]{2,1,0:T(8,128)(2,1)}), bf16[8,12,4096]{2,1,0:T(8,128)(2,1)S(1)}, u32[]{:S(2)}, u32[]{:S(2)}) async-start(bf16[8,12,4096]{2,1,0:T(8,128)(2,1)} %stack.5), calls=%async_computation.1 | async-start | bytes 2097152 | tf_op jit(solution)/shard_map/all_to_all | solution.py:9
